TPU v7x, 16 devices: a 4x2x1 block of a 4x4x8 slice. The times are simulated.
16 devices in a mesh: mat: 2 (over y, z), dp: 8 (over x, core).
Axes of the slice: x: 4, y: 2, z: 1, core: 2. Of those that a mesh axis runs over, the one named last changes fastest.
The devices are a block of a 4x4x8 slice.
Arguments:
- a_mat: bfloat16 [9216, 65536], P('mat', 'dp'), parts along dimension 0
Outputs:
- output: float32 [16, 5, 576, 576], P(('mat', 'dp')), parts along dimension 0
There are 2 independent parts. A program takes and returns all parts, laid end to end along the dimension named above; each array names one.
All inputs are finite; a program needn't handle non-finite values.
Results may differ from a plain program's by a relative error of at most 0.001.
Values are sent between devices in bfloat16 or wider.
A program may use at most 768 MiB of HBM per device.

v0:
```python
import jax
import jax.numpy as jnp
from jax import lax
from jax.sharding import PartitionSpec as P


def packed_partial(blocks):
    groups = blocks.shape[0]
    blk_rows = blocks.shape[1]
    half = groups // 2
    slots = half + 1
    doubled = jnp.concatenate([blocks, blocks], axis=0)
    dev_ids = lax.broadcasted_iota(jnp.int32, (groups, 1, 1), 0)

    def slot_step(slot, packed):
        partner = lax.dynamic_slice_in_dim(doubled, groups - slot, groups, axis=0)
        block_prod = jnp.einsum('gik,gjk->gij', blocks, partner, preferred_element_type=jnp.float32)
        flipped = jnp.where(dev_ids < slot, jnp.swapaxes(block_prod, 1, 2), block_prod)
        keep_mask = jnp.logical_or(slot < half, dev_ids < half)
        return lax.dynamic_update_index_in_dim(packed, jnp.where(keep_mask, flipped, 0.0), slot, axis=1)

    packed = jnp.zeros((groups, slots, blk_rows, blk_rows), jnp.float32)
    return lax.fori_loop(0, slots, slot_step, packed)


def solution(mesh):
    groups = mesh.shape['dp']

    def local_gram(a_local):
        n_rows, local_cols = a_local.shape
        blocks = a_local.reshape(groups, n_rows // groups, local_cols)
        return lax.psum_scatter(packed_partial(blocks), 'dp', scatter_dimension=0, tiled=True)

    return jax.shard_map(local_gram, mesh=mesh, in_specs=(P('mat', 'dp'),), out_specs=P(('mat', 'dp')), check_vma=False)
```

profile of v0, /device:TPU:117, one launch (start us, length us, event | category | flops | bytes accessed | tf_op | source)
XLA Modules:
  0.0 887.8 jit_solution(12248804404688651725)
XLA Ops:
  6.5 0.0 reduce-scatter.2.cloned.1.call-start
  6.6 98.7 %pad_maximum_fusion = bf16[16,576,8192]{2,1,0:T(8,128)(2,1)} fusion(bf16[8,576,8192]{2,1,0:T(8,128)(2,1)} %bitcast), kind=kLoop, calls=%fused_computation.9 | loop fusion | flops 75497472 | bytes 226492416 | tf_op jit(solution)/shard_map/concatenate | solution.py:12
  105.3 488.7 %while.17 = (s32[]{:T(128)}, f32[8,5,576,576]{3,2,1,0:T(8,128)}, bf16[16,576,8192]{2,1,0:T(8,128)(2,1)}, bf16[8,576,8192]{2,1,0:T(8,128)(2,1)}, s32[]{:T(128)}, ...) while((s32[]{:T(128)}, f32[8,5,576,576]{3,2,1,0:T(8,128)}, ...), condition=%wide.region_1.2_spmd.clone.clone, body=%wide.region_0.1_spmd.clone.clone.sunk | while | flops 43491852288 | bytes 218235600 | solution.py:23
  105.3 72.2 %fusion.15 = f32[8,576,576]{2,1,0:T(8,128)} fusion(bf16[8,576,8192]{2,1,0:T(8,128)(2,1)} %get-tuple-element.225, bf16[16,576,8192]{2,1,0:T(8,128)(2,1)} %get-tuple-element.224, s32[]{:T(128)S(6)} %select_n.60), kind=kOutput, calls=%fused_computation.1.clone.2 | convolution fusion | flops 43486543872 | bytes 161611776 | tf_op jit(solution)/shard_map/while/body/eval_jaxpr/gik,gjk->gij/dot_general | solution.py:17
  177.5 12.3 %copy.7 = f32[8,576,576]{1,2,0:T(8,128)} copy(f32[8,576,576]{2,1,0:T(8,128)} %fusion.15) | data formatting | bytes 21233664 | tf_op jit(solution)/shard_map/while/body/eval_jaxpr/gik,gjk->gij/dot_general | solution.py:17
  189.8 13.3 %bitcast_dynamic-update-slice_fusion.2 = f32[8,5,576,576]{3,2,1,0:T(8,128)} fusion(f32[8,5,576,576]{3,2,1,0:T(8,128)} %get-tuple-element.214, s32[]{:T(128)} %get-tuple-element.213, f32[8,576,576]{2,1,0:T(8,128)} %fusion.15, f32[8,576,576]{1,2,0:T(8,128)} %copy.7, pred[8]{0:T(512)(128)(4,1)S(1)} %get-tuple-element.202, ...), kind=kLoop, calls=%fused_computation.3.clone.1 | loop fusion | flops 5308416 | bytes 35389968 | tf_op jit(solution)/shard_map/while/body/eval_jaxpr/jit(dynamic_update_index_in_dim)/dynamic_update_slice | solution.py:20
  203.1 72.2 %fusion.15 = f32[8,576,576]{2,1,0:T(8,128)} fusion(bf16[8,576,8192]{2,1,0:T(8,128)(2,1)} %get-tuple-element.225, bf16[16,576,8192]{2,1,0:T(8,128)(2,1)} %get-tuple-element.224, s32[]{:T(128)S(6)} %select_n.60), kind=kOutput, calls=%fused_computation.1.clone.2 | convolution fusion | flops 43486543872 | bytes 161611776 | tf_op jit(solution)/shard_map/while/body/eval_jaxpr/gik,gjk->gij/dot_general | solution.py:17
  275.3 12.3 %copy.7 = f32[8,576,576]{1,2,0:T(8,128)} copy(f32[8,576,576]{2,1,0:T(8,128)} %fusion.15) | data formatting | bytes 21233664 | tf_op jit(solution)/shard_map/while/body/eval_jaxpr/gik,gjk->gij/dot_general | solution.py:17
  287.6 13.2 %bitcast_dynamic-update-slice_fusion.2 = f32[8,5,576,576]{3,2,1,0:T(8,128)} fusion(f32[8,5,576,576]{3,2,1,0:T(8,128)} %get-tuple-element.214, s32[]{:T(128)} %get-tuple-element.213, f32[8,576,576]{2,1,0:T(8,128)} %fusion.15, f32[8,576,576]{1,2,0:T(8,128)} %copy.7, pred[8]{0:T(512)(128)(4,1)S(1)} %get-tuple-element.202, ...), kind=kLoop, calls=%fused_computation.3.clone.1 | loop fusion | flops 5308416 | bytes 35389968 | tf_op jit(solution)/shard_map/while/body/eval_jaxpr/jit(dynamic_update_index_in_dim)/dynamic_update_slice | solution.py:20
  300.8 72.2 %fusion.15 = f32[8,576,576]{2,1,0:T(8,128)} fusion(bf16[8,576,8192]{2,1,0:T(8,128)(2,1)} %get-tuple-element.225, bf16[16,576,8192]{2,1,0:T(8,128)(2,1)} %get-tuple-element.224, s32[]{:T(128)S(6)} %select_n.60), kind=kOutput, calls=%fused_computation.1.clone.2 | convolution fusion | flops 43486543872 | bytes 161611776 | tf_op jit(solution)/shard_map/while/body/eval_jaxpr/gik,gjk->gij/dot_general | solution.py:17
  373.0 12.3 %copy.7 = f32[8,576,576]{1,2,0:T(8,128)} copy(f32[8,576,576]{2,1,0:T(8,128)} %fusion.15) | data formatting | bytes 21233664 | tf_op jit(solution)/shard_map/while/body/eval_jaxpr/gik,gjk->gij/dot_general | solution.py:17
  385.3 13.2 %bitcast_dynamic-update-slice_fusion.2 = f32[8,5,576,576]{3,2,1,0:T(8,128)} fusion(f32[8,5,576,576]{3,2,1,0:T(8,128)} %get-tuple-element.214, s32[]{:T(128)} %get-tuple-element.213, f32[8,576,576]{2,1,0:T(8,128)} %fusion.15, f32[8,576,576]{1,2,0:T(8,128)} %copy.7, pred[8]{0:T(512)(128)(4,1)S(1)} %get-tuple-element.202, ...), kind=kLoop, calls=%fused_computation.3.clone.1 | loop fusion | flops 5308416 | bytes 35389968 | tf_op jit(solution)/shard_map/while/body/eval_jaxpr/jit(dynamic_update_index_in_dim)/dynamic_update_slice | solution.py:20
  398.5 72.2 %fusion.15 = f32[8,576,576]{2,1,0:T(8,128)} fusion(bf16[8,576,8192]{2,1,0:T(8,128)(2,1)} %get-tuple-element.225, bf16[16,576,8192]{2,1,0:T(8,128)(2,1)} %get-tuple-element.224, s32[]{:T(128)S(6)} %select_n.60), kind=kOutput, calls=%fused_computation.1.clone.2 | convolution fusion | flops 43486543872 | bytes 161611776 | tf_op jit(solution)/shard_map/while/body/eval_jaxpr/gik,gjk->gij/dot_general | solution.py:17
  470.7 12.3 %copy.7 = f32[8,576,576]{1,2,0:T(8,128)} copy(f32[8,576,576]{2,1,0:T(8,128)} %fusion.15) | data formatting | bytes 21233664 | tf_op jit(solution)/shard_map/while/body/eval_jaxpr/gik,gjk->gij/dot_general | solution.py:17
  483.0 13.2 %bitcast_dynamic-update-slice_fusion.2 = f32[8,5,576,576]{3,2,1,0:T(8,128)} fusion(f32[8,5,576,576]{3,2,1,0:T(8,128)} %get-tuple-element.214, s32[]{:T(128)} %get-tuple-element.213, f32[8,576,576]{2,1,0:T(8,128)} %fusion.15, f32[8,576,576]{1,2,0:T(8,128)} %copy.7, pred[8]{0:T(512)(128)(4,1)S(1)} %get-tuple-element.202, ...), kind=kLoop, calls=%fused_computation.3.clone.1 | loop fusion | flops 5308416 | bytes 35389968 | tf_op jit(solution)/shard_map/while/body/eval_jaxpr/jit(dynamic_update_index_in_dim)/dynamic_update_slice | solution.py:20
  496.2 72.2 %fusion.15 = f32[8,576,576]{2,1,0:T(8,128)} fusion(bf16[8,576,8192]{2,1,0:T(8,128)(2,1)} %get-tuple-element.225, bf16[16,576,8192]{2,1,0:T(8,128)(2,1)} %get-tuple-element.224, s32[]{:T(128)S(6)} %select_n.60), kind=kOutput, calls=%fused_computation.1.clone.2 | convolution fusion | flops 43486543872 | bytes 161611776 | tf_op jit(solution)/shard_map/while/body/eval_jaxpr/gik,gjk->gij/dot_general | solution.py:17
  568.4 12.3 %copy.7 = f32[8,576,576]{1,2,0:T(8,128)} copy(f32[8,576,576]{2,1,0:T(8,128)} %fusion.15) | data formatting | bytes 21233664 | tf_op jit(solution)/shard_map/while/body/eval_jaxpr/gik,gjk->gij/dot_general | solution.py:17
  580.7 13.3 %bitcast_dynamic-update-slice_fusion.2 = f32[8,5,576,576]{3,2,1,0:T(8,128)} fusion(f32[8,5,576,576]{3,2,1,0:T(8,128)} %get-tuple-element.214, s32[]{:T(128)} %get-tuple-element.213, f32[8,576,576]{2,1,0:T(8,128)} %fusion.15, f32[8,576,576]{1,2,0:T(8,128)} %copy.7, pred[8]{0:T(512)(128)(4,1)S(1)} %get-tuple-element.202, ...), kind=kLoop, calls=%fused_computation.3.clone.1 | loop fusion | flops 5308416 | bytes 35389968 | tf_op jit(solution)/shard_map/while/body/eval_jaxpr/jit(dynamic_update_index_in_dim)/dynamic_update_slice | solution.py:20
  594.0 0.1 reduce-scatter.2.cloned.1.call-update
  594.1 286.9 %reduce-scatter.2.cloned.1.call-done = f32[1,5,576,576]{3,2,1,0:T(8,128)} async-done(((f32[8,5,576,576]{3,2,1,0:T(8,128)}), f32[1,5,576,576]{3,2,1,0:T(8,128)}) %reduce-scatter.2.cloned.1.call-update) | async-done | bytes 6635536 | tf_op jit(solution)/shard_map/reduce_scatter | solution.py:32
  (6 shorter events, 0.0 us)
Async XLA Ops:
  6.5 874.4 %reduce-scatter.2.cloned.1.call-start = ((), (), s32[]{:S(2)}) async-start(), calls=%async_computation.1 | async-start | bytes 66355200 | tf_op jit(solution)/shard_map/reduce_scatter | solution.py:32
Sparse Core Ops, SparseCore 0:
  594.2 286.7 reduce-scatter.1
where the time goes:
time: 891 us; the launch traced here: 888 us
  matrix products  361 us (41%)
  waiting for transfers between devices  287 us (32%)
  other arithmetic  165 us (19%)
  local copies, waits for them, and re-layouts  61.5 us (7%)
  between operations  13.4 us (2%)
    dot_general x5, matrix products, slot_step(): jnp.einsum('gik,gjk->gij', blocks, partner, preferred_element_type=jnp.fl...  361 us
    reduce_scatter x1, waiting for transfers between devices, local_gram(): lax.psum_scatter(packed_partial(blocks), 'dp', scatter_dimension=0, tiled...  287 us
    concatenate x1, other arithmetic, packed_partial(): doubled = jnp.concatenate([blocks, blocks], axis=0)  98.7 us
    dynamic_update_slice x5, other arithmetic, slot_step(): lax.dynamic_update_index_in_dim(packed, jnp.where(keep_mask, flipped, 0.0...  66.2 us
    dot_general x5, local copies, waits for them, and re-layouts, slot_step(): jnp.einsum('gik,gjk->gij', blocks, partner, preferred_element_type=jnp.fl...  61.5 us
  transfers between devices with their start and end apart: 1, of which 1 were waited for; matrix products, arithmetic and copies ran while one was open for 0% of the time, Pallas kernels for 0%

commit v1 on v0

v1 whole, which is shorter than its diff:
```python
import functools

import jax
import jax.numpy as jnp
from jax import lax
from jax.experimental import pallas as pl
from jax.experimental.pallas import tpu as pltpu
from jax.sharding import PartitionSpec as P

MAIN = 512
DLAND = 3
RING = 14


def select(index, values):
    out = jnp.int32(values[-1])
    for k in range(len(values) - 2, -1, -1):
        out = jnp.where(index == k, jnp.int32(values[k]), out)
    return out


def kernel(groups, a_ref, out_ref, land, lhs, rhs, res, dland, sbuf, srem, rbuf, remf, fin,
           lhs_sem, rhs_sem, dsend, drecv, credit, ssend, rsend, lrecv, load_sem, fin_sem):
    chips = groups // 2
    half = groups // 2
    rows = lhs.shape[1]
    hrows = rows // 2
    rest = rows - MAIN
    visits = groups
    far = visits - 2
    strips = half + 2
    total = visits + groups * (half + 1) - half
    me = lax.axis_index('dp')
    x, c = me // 2, me % 2
    partner = x * 2 + (1 - c)

    def dest(v):
        off = select(v, (2, 2, 1, chips - 1, 1, chips - 1, 0, 0))
        core = select(v, (0, 1, 0, 0, 1, 1, 0, 1))
        chip = (x + off) % chips
        return chip * 2 + core, core

    def slots_of(p):
        return jnp.where(p < half, half + 1, half)

    def via_plus(p, s):
        mains = select(p, (2, 2, 3, 4, 3, 2, 1, 2))
        return jnp.where(s == 0, select(p, (0, 1, 0, 0, 0, 1, 0, 0)) == 1, s - 1 < mains)

    def widths(p, s):
        wide = p < half
        return (
            (MAIN, s > 0),
            (384, jnp.logical_and(s == 0, wide)),
            (256, jnp.logical_and(s == 0, jnp.logical_not(wide))),
        )

    def on_route(v, p, s):
        plus = via_plus(p, s)
        right = jnp.logical_or(v == 2, v == 4)
        there = jnp.where(right, jnp.logical_not(plus), plus)
        return jnp.logical_and(jnp.logical_and(v >= 2, v < far), there)

    def first_slot(side, core, s):
        return (side * 2 + core) * strips + s

    def last_slot(side, part, s):
        return (4 + side * 2 + part) * strips + s

    def start_lhs(v):
        p, _ = dest(v)
        pltpu.make_async_copy(
            a_ref.at[pl.ds(pl.multiple_of(p * rows, 64), rows)], lhs.at[v % 2], lhs_sem.at[v % 2]
        ).start()

    def start_rhs(v, s, slot):
        p, _ = dest(v)

        @pl.when(s > 0)
        def _():
            q = (p - (s - 1) + groups) % groups
            pltpu.make_async_copy(
                a_ref.at[pl.ds(pl.multiple_of(q * rows, 64), MAIN)], rhs.at[slot], rhs_sem.at[slot]
            ).start()

        def piece(t, k):
            q = (p - t + groups) % groups
            pltpu.make_async_copy(
                a_ref.at[pl.ds(pl.multiple_of(q * rows + MAIN, 64), rest)],
                rhs.at[slot, pl.ds(k * rest, rest)],
                rhs_sem.at[slot],
            ).start()

        @pl.when(s == 0)
        def _():
            for t in range(half):
                piece(t, t)

            @pl.when(p < half)
            def _():
                piece(half, half)
                piece(0, half + 1)

    def signal_credit(kr, received):
        @pl.when(kr + DLAND < received)
        def _():
            pl.semaphore_signal(credit.at[kr % DLAND], inc=1, device_id={'dp': partner}, device_id_type=pl.DeviceIdType.MESH)

    own = me
    received = total - (slots_of(own) + 1)

    def before(v, s):
        p, core = dest(v)
        for width, cond in widths(p, s):
            @pl.when(jnp.logical_and(cond, on_route(v, p, s)))
            def _():
                side = jnp.where(jnp.logical_or(v == 2, v == 4), 0, 1)
                k = first_slot(side, core, s)
                block = land.at[k, :, pl.ds(0, width)]
                pltpu.make_async_copy(block, block, lrecv.at[k]).wait()
                pltpu.make_async_copy(block, rbuf.at[0, pl.ds(0, hrows), pl.ds(0, width)], load_sem.at[0]).start()

            @pl.when(jnp.logical_and(cond, jnp.logical_and(v >= far, core == c)))
            def _():
                for side in range(2):
                    for part in range(2):
                        k = last_slot(side, part, s)
                        block = land.at[k, :, pl.ds(0, width)]
                        pltpu.make_async_copy(block, block, lrecv.at[k]).wait()
                        pltpu.make_async_copy(
                            block,
                            rbuf.at[side, pl.ds(part * hrows, hrows), pl.ds(0, width)],
                            load_sem.at[side * 2 + part],
                        ).start()

    def after(v, s, slot, kt, kr):
        p, core = dest(v)
        k = kr % DLAND
        mine = pl.ds(pl.multiple_of(c * hrows, 8), hrows)
        other = pl.ds(pl.multiple_of((1 - c) * hrows, 8), hrows)
        plus = via_plus(p, s)
        right = jnp.logical_or(v == 2, v == 4)
        routed = on_route(v, p, s)
        hop = jnp.where(plus, (x + chips - 1) % chips, (x + 1) % chips)
        target = jnp.where(v < 2, hop * 2 + c, p)
        place = jnp.where(
            v < 2,
            first_slot(jnp.where(plus, 1, 0), core, s),
            last_slot(jnp.where(right, 0, 1), c, s),
        )

        for width, cond in widths(p, s):
            cols = pl.ds(0, width)

            @pl.when(jnp.logical_and(cond, v < far))
            def _():
                got = dland.at[k, pl.ds(0, hrows), cols]
                pltpu.make_async_copy(got, got, drecv.at[k]).wait()

                def send(buf, sem):
                    val = res[slot, mine, cols] + dland[k, pl.ds(0, hrows), cols]

                    @pl.when(routed)
                    def _():
                        add = rbuf.at[0, pl.ds(0, hrows), cols]
                        pltpu.make_async_copy(add, add, load_sem.at[0]).wait()
                        buf[...] = res[slot, mine, cols] + dland[k, pl.ds(0, hrows), cols] + rbuf[0, pl.ds(0, hrows), cols]

                    @pl.when(jnp.logical_not(routed))
                    def _():
                        buf[...] = res[slot, mine, cols] + dland[k, pl.ds(0, hrows), cols]

                    pltpu.make_async_remote_copy(
                        src_ref=buf,
                        dst_ref=land.at[place, :, cols],
                        send_sem=sem,
                        recv_sem=lrecv.at[place],
                        device_id={'dp': target},
                        device_id_type=pl.DeviceIdType.MESH,
                    ).start()

                if width == MAIN:
                    ring = kt % RING

                    @pl.when(kt >= RING)
                    def _():
                        pltpu.make_async_copy(sbuf.at[ring], sbuf.at[ring], ssend.at[ring]).wait()

                    send(sbuf.at[ring], ssend.at[ring])
                else:
                    send(srem.at[v, :, cols], rsend.at[v])
                sent = res.at[slot, other, cols]
                pltpu.make_async_copy(sent, sent, dsend.at[slot]).wait()
                signal_credit(kr, received)

            @pl.when(jnp.logical_and(cond, jnp.logical_and(v >= far, core == c)))
            def _():
                got = dland.at[k, :, cols]
                pltpu.make_async_copy(got, got, drecv.at[k]).wait()
                for side in range(2):
                    for part in range(2):
                        add = rbuf.at[side, pl.ds(part * hrows, hrows), cols]
                        pltpu.make_async_copy(add, add, load_sem.at[side * 2 + part]).wait()

                def whole():
                    return res[slot, :, cols] + dland[k, :, cols] + (rbuf[0, :, cols] + rbuf[1, :, cols])

                if width != MAIN:
                    remf[:, cols] = whole()
                else:
                    t = s - 1

                    @pl.when(t > 0)
                    def _():
                        pltpu.make_async_copy(fin, fin, fin_sem).wait()

                    @pl.when(t <= p)
                    def _():
                        fin[:, cols] = whole()
                        for i in range(half + 1):
                            @pl.when(t == i)
                            def _():
                                fin[:, pl.ds(MAIN, rest)] = remf[:, pl.ds(i * rest, rest)]

                    @pl.when(t > p)
                    def _():
                        fin[pl.ds(0, MAIN), :] = whole().T
                        for i in range(half + 1):
                            @pl.when(t == i)
                            def _():
                                pair = remf[:, pl.ds(i // 2 * 128, 128)].T
                                fin[pl.ds(MAIN, rest), :] = pair[i % 2 * rest:(i % 2 + 1) * rest]

                    pltpu.make_async_copy(fin, out_ref.at[t], fin_sem).start()
                signal_credit(kr, received)

            @pl.when(jnp.logical_and(cond, jnp.logical_and(v >= far, core != c)))
            def _():
                sent = res.at[slot, :, cols]
                pltpu.make_async_copy(sent, sent, dsend.at[slot]).wait()

        takes = jnp.logical_or(v < far, core == c)
        kr = kr + jnp.where(takes, 1, 0)
        kt = kt + jnp.where(jnp.logical_and(v < far, s > 0), 1, 0)
        return kt, kr

    start_lhs(jnp.int32(0))
    start_rhs(jnp.int32(0), jnp.int32(0), 0)

    barrier = pltpu.get_barrier_semaphore()
    peers = [partner]
    for step in (1, chips - 1):
        for core in range(2):
            peers.append((x + step) % chips * 2 + core)
    for peer in peers:
        pl.semaphore_signal(barrier, inc=1, device_id={'dp': peer}, device_id_type=pl.DeviceIdType.MESH)
    pl.semaphore_wait(barrier, len(peers))

    @pl.when(own >= half)
    def _():
        fin[...] = jnp.zeros_like(fin)
        pad = pltpu.make_async_copy(fin, out_ref.at[half], fin_sem)
        pad.start()
        pad.wait()

    def step(g, carry):
        v, s, pv, ps, kt, ks, kr = carry
        p, core = dest(v)
        slot = g % 2
        nt = slots_of(p)
        end = s == nt
        nv = jnp.where(end, v + 1, v)
        ns = jnp.where(end, 0, s + 1)

        for width, cond in widths(p, s):
            @pl.when(cond)
            def _():
                block = rhs.at[slot, pl.ds(0, width)]
                pltpu.make_async_copy(block, block, rhs_sem.at[slot]).wait()

        @pl.when(g + 1 < total)
        def _():
            start_rhs(nv, ns, 1 - slot)

        @pl.when(s == 0)
        def _():
            pltpu.make_async_copy(lhs.at[v % 2], lhs.at[v % 2], lhs_sem.at[v % 2]).wait()

            @pl.when(v + 1 < visits)
            def _():
                start_lhs(v + 1)

        @pl.when(g > 0)
        def _():
            before(pv, ps)

        for width, cond in widths(p, s):
            @pl.when(cond)
            def _():
                res[slot, :, pl.ds(0, width)] = lax.dot_general(
                    lhs[v % 2], rhs[slot, pl.ds(0, width)], (((1,), (1,)), ((), ())),
                    preferred_element_type=jnp.float32,
                )

        gives = jnp.logical_or(v < far, core != c)
        k = ks % DLAND

        @pl.when(jnp.logical_and(gives, ks >= DLAND))
        def _():
            pl.semaphore_wait(credit.at[k], 1)

        for width, cond in widths(p, s):
            cols = pl.ds(0, width)

            def give(src_rows, dst_rows):
                pltpu.make_async_remote_copy(
                    src_ref=res.at[slot, src_rows, cols],
                    dst_ref=dland.at[k, dst_rows, cols],
                    send_sem=dsend.at[slot],
                    recv_sem=drecv.at[k],
                    device_id={'dp': partner},
                    device_id_type=pl.DeviceIdType.MESH,
                ).start()

            @pl.when(jnp.logical_and(cond, v < far))
            def _():
                give(pl.ds(pl.multiple_of((1 - c) * hrows, 8), hrows), pl.ds(0, hrows))

            @pl.when(jnp.logical_and(cond, jnp.logical_and(v >= far, core != c)))
            def _():
                give(pl.ds(0, rows), pl.ds(0, rows))

        ks = ks + jnp.where(gives, 1, 0)

        @pl.when(g > 0)
        def _():
            after(pv, ps, 1 - slot, kt, kr)

        takes = jnp.logical_and(g > 0, jnp.logical_or(pv < far, dest(pv)[1] == c))
        kr = kr + jnp.where(takes, 1, 0)
        kt = kt + jnp.where(jnp.logical_and(g > 0, jnp.logical_and(pv < far, ps > 0)), 1, 0)
        return nv, ns, v, s, kt, ks, kr

    zero = jnp.int32(0)
    _, _, pv, ps, kt, ks, kr = lax.fori_loop(0, total, step, (zero,) * 7)
    before(pv, ps)
    after(pv, ps, (total - 1) % 2, kt, kr)

    for ring in range(RING):
        pltpu.make_async_copy(sbuf.at[ring], sbuf.at[ring], ssend.at[ring]).wait()
    for v in range(far):
        p, _ = dest(jnp.int32(v))
        for width, cond in widths(p, jnp.int32(0))[1:]:
            @pl.when(cond)
            def _():
                block = srem.at[v, :, pl.ds(0, width)]
                pltpu.make_async_copy(block, block, rsend.at[v]).wait()
    pltpu.make_async_copy(fin, fin, fin_sem).wait()


def solution(mesh):
    groups = mesh.shape['dp']

    def local_gram(a_local):
        n_rows, cols = a_local.shape
        rows = n_rows // groups
        hrows = rows // 2
        slots = groups // 2 + 1
        landing = 8 * (slots + 1)
        out, _ = pl.pallas_call(
            functools.partial(kernel, groups),
            out_shape=(
                jax.ShapeDtypeStruct((slots, rows, rows), jnp.float32),
                jax.ShapeDtypeStruct((landing, hrows, MAIN), jnp.float32),
            ),
            in_specs=[pl.BlockSpec(memory_space=pl.ANY)],
            out_specs=(pl.BlockSpec(memory_space=pl.ANY), pl.BlockSpec(memory_space=pl.ANY)),
            scratch_shapes=[
                pltpu.VMEM((2, rows, cols), jnp.bfloat16),
                pltpu.VMEM((2, MAIN, cols), jnp.bfloat16),
                pltpu.VMEM((2, rows, MAIN), jnp.float32),
                pltpu.VMEM((DLAND, rows, MAIN), jnp.float32),
                pltpu.VMEM((RING, hrows, MAIN), jnp.float32),
                pltpu.VMEM((groups - 2, hrows, 384), jnp.float32),
                pltpu.VMEM((2, rows, MAIN), jnp.float32),
                pltpu.VMEM((rows, 384), jnp.float32),
                pltpu.VMEM((rows, rows), jnp.float32),
                pltpu.SemaphoreType.DMA((2,)),
                pltpu.SemaphoreType.DMA((2,)),
                pltpu.SemaphoreType.DMA((2,)),
                pltpu.SemaphoreType.DMA((DLAND,)),
                pltpu.SemaphoreType.REGULAR((DLAND,)),
                pltpu.SemaphoreType.DMA((RING,)),
                pltpu.SemaphoreType.DMA((groups - 2,)),
                pltpu.SemaphoreType.DMA((landing,)),
                pltpu.SemaphoreType.DMA((4,)),
                pltpu.SemaphoreType.DMA,
            ],
            compiler_params=pltpu.CompilerParams(
                collective_id=0, has_side_effects=True, vmem_limit_bytes=67_000_000
            ),
            name='gram_reduce',
        )(a_local)
        return out.reshape(slots, rows, rows)[None]

    return jax.shard_map(local_gram, mesh=mesh, in_specs=(P('mat', 'dp'),), out_specs=P(('mat', 'dp')), check_vma=False)
```

time: 891 us -> 267 us (0.30)
  the two profiles are of different devices: /device:TPU:117 before, /device:TPU:123 now
where the time goes in v1:
time: 267 us
  Pallas kernels  261 us (98%)
  local copies, waits for them, and re-layouts  6.63 us (2%)
    pallas_call x1, Pallas kernels, local_gram(): pl.pallas_call(functools.partial(kernel, groups), out_shape=(jax.ShapeDty...  261 us
    unnamed x1, local copies, waits for them, and re-layouts  6.63 us

profile of v1, /device:TPU:123, one launch (start us, length us, event | category | flops | bytes accessed | tf_op | source)
XLA Modules:
  0.0 267.3 jit_solution(13018580855573208875)
XLA Ops:
  0.0 260.7 %gram_reduce.1 = (f32[5,576,576]{2,1,0:T(8,128)}, f32[48,288,512]{2,1,0:T(8,128)}) custom-call(bf16[4608,8192]{1,0:T(8,128)(2,1)} %a_ref.1), custom_call_target="tpu_custom_call" | custom-call | tf_op jit(solution)/shard_map/gram_reduce/pallas_call | solution.py:370
  260.7 6.6 %copy.3 = f32[1,5,576,576]{3,2,1,0:T(8,128)} copy(f32[1,5,576,576]{3,2,1,0:T(8,128)} %bitcast.1) | data formatting | bytes 13271040

commit v2 on v1

--- a/solution.py
+++ b/solution.py
@@ -34,8 +34,12 @@
     x, c = me // 2, me % 2
     partner = x * 2 + (1 - c)
 
+    def rightward(v):
+        return (v % 2 == 0) == ((x + 1) % chips >= chips // 2)
+
     def dest(v):
-        off = select(v, (2, 2, 1, chips - 1, 1, chips - 1, 0, 0))
+        side = jnp.where(rightward(v), 1, chips - 1)
+        off = jnp.where(v < 2, 2, jnp.where(v < far, side, 0))
         core = select(v, (0, 1, 0, 0, 1, 1, 0, 1))
         chip = (x + off) % chips
         return chip * 2 + core, core
@@ -44,8 +48,24 @@
         return jnp.where(p < half, half + 1, half)
 
     def via_plus(p, s):
-        mains = select(p, (2, 2, 3, 4, 3, 2, 1, 2))
-        return jnp.where(s == 0, select(p, (0, 1, 0, 0, 0, 1, 0, 0)) == 1, s - 1 < mains)
+        masks = select(p, (0b010100, 0b010101, 0b101010, 0b110110, 0b010110, 0b001011, 0b000100, 0b010100))
+        return masks // select(s, (1, 2, 4, 8, 16, 32)) % 2 == 1
+
+    def strip_at(v, i):
+        return jnp.where(v < far, jnp.where(i == slots_of(dest(v)[0]), 0, i + 1), i)
+
+    def following(v, s):
+        nt = slots_of(dest(v)[0])
+        paired = jnp.logical_and(v >= 2, v < far)
+        first = v % 2 == 0
+        mate = jnp.where(first, v + 1, v - 1)
+        mate_s = jnp.where(first, s, s + 1)
+        take_mate = jnp.logical_and(paired, mate_s <= slots_of(dest(mate)[0]))
+        more = s < nt
+        later = jnp.where(jnp.logical_and(paired, first), v + 2, v + 1)
+        nv = jnp.where(take_mate, mate, jnp.where(more, v, later))
+        ns = jnp.where(take_mate, mate_s, jnp.where(more, s + 1, 0))
+        return nv, ns
 
     def widths(p, s):
         wide = p < half
@@ -57,7 +77,7 @@
 
     def on_route(v, p, s):
         plus = via_plus(p, s)
-        right = jnp.logical_or(v == 2, v == 4)
+        right = rightward(v)
         there = jnp.where(right, jnp.logical_not(plus), plus)
         return jnp.logical_and(jnp.logical_and(v >= 2, v < far), there)
 
@@ -114,7 +134,7 @@
         for width, cond in widths(p, s):
             @pl.when(jnp.logical_and(cond, on_route(v, p, s)))
             def _():
-                side = jnp.where(jnp.logical_or(v == 2, v == 4), 0, 1)
+                side = jnp.where(rightward(v), 0, 1)
                 k = first_slot(side, core, s)
                 block = land.at[k, :, pl.ds(0, width)]
                 pltpu.make_async_copy(block, block, lrecv.at[k]).wait()
@@ -139,7 +159,7 @@
         mine = pl.ds(pl.multiple_of(c * hrows, 8), hrows)
         other = pl.ds(pl.multiple_of((1 - c) * hrows, 8), hrows)
         plus = via_plus(p, s)
-        right = jnp.logical_or(v == 2, v == 4)
+        right = rightward(v)
         routed = on_route(v, p, s)
         hop = jnp.where(plus, (x + chips - 1) % chips, (x + 1) % chips)
         target = jnp.where(v < 2, hop * 2 + c, p)
@@ -245,7 +265,7 @@
         return kt, kr
 
     start_lhs(jnp.int32(0))
-    start_rhs(jnp.int32(0), jnp.int32(0), 0)
+    start_rhs(jnp.int32(0), jnp.int32(1), 0)
 
     barrier = pltpu.get_barrier_semaphore()
     peers = [partner]
@@ -264,13 +284,11 @@
         pad.wait()
 
     def step(g, carry):
-        v, s, pv, ps, kt, ks, kr = carry
+        v, i, pv, pi, kt, ks, kr = carry
         p, core = dest(v)
+        s, ps = strip_at(v, i), strip_at(pv, pi)
         slot = g % 2
-        nt = slots_of(p)
-        end = s == nt
-        nv = jnp.where(end, v + 1, v)
-        ns = jnp.where(end, 0, s + 1)
+        nv, ni = following(v, i)
 
         for width, cond in widths(p, s):
             @pl.when(cond)
@@ -280,15 +298,19 @@
 
         @pl.when(g + 1 < total)
         def _():
-            start_rhs(nv, ns, 1 - slot)
-
-        @pl.when(s == 0)
+            start_rhs(nv, strip_at(nv, ni), 1 - slot)
+
+        @pl.when(g == 1)
+        def _():
+            start_lhs(jnp.int32(1))
+
+        @pl.when(jnp.logical_and(g > 0, jnp.logical_and(pi == slots_of(dest(pv)[0]), pv + 2 < visits)))
+        def _():
+            start_lhs(pv + 2)
+
+        @pl.when(i == 0)
         def _():
             pltpu.make_async_copy(lhs.at[v % 2], lhs.at[v % 2], lhs_sem.at[v % 2]).wait()
-
-            @pl.when(v + 1 < visits)
-            def _():
-                start_lhs(v + 1)
 
         @pl.when(g > 0)
         def _():
@@ -339,10 +361,11 @@
         takes = jnp.logical_and(g > 0, jnp.logical_or(pv < far, dest(pv)[1] == c))
         kr = kr + jnp.where(takes, 1, 0)
         kt = kt + jnp.where(jnp.logical_and(g > 0, jnp.logical_and(pv < far, ps > 0)), 1, 0)
-        return nv, ns, v, s, kt, ks, kr
+        return nv, ni, v, i, kt, ks, kr
 
     zero = jnp.int32(0)
-    _, _, pv, ps, kt, ks, kr = lax.fori_loop(0, total, step, (zero,) * 7)
+    _, _, pv, pi, kt, ks, kr = lax.fori_loop(0, total, step, (zero,) * 7)
+    ps = strip_at(pv, pi)
     before(pv, ps)
     after(pv, ps, (total - 1) % 2, kt, kr)
 

time: 267 us -> 281 us (1.052)
  the two profiles are of different devices: /device:TPU:123 before, /device:TPU:113 now
where the time goes in v2:
time: 281 us
  Pallas kernels  274 us (98%)
  local copies, waits for them, and re-layouts  6.63 us (2%)
    pallas_call x1, Pallas kernels, local_gram(): pl.pallas_call(functools.partial(kernel, groups), out_shape=(jax.ShapeDty...  274 us
    unnamed x1, local copies, waits for them, and re-layouts  6.63 us

profile of v2, /device:TPU:113, one launch (start us, length us, event | category | flops | bytes accessed | tf_op | source)
XLA Modules:
  0.0 280.6 jit_solution(17975903849531967857)
XLA Ops:
  0.0 273.9 %gram_reduce.1 = (f32[5,576,576]{2,1,0:T(8,128)}, f32[48,288,512]{2,1,0:T(8,128)}) custom-call(bf16[4608,8192]{1,0:T(8,128)(2,1)} %a_ref.1), custom_call_target="tpu_custom_call" | custom-call | tf_op jit(solution)/shard_map/gram_reduce/pallas_call | solution.py:393
  274.0 6.6 %copy.3 = f32[1,5,576,576]{3,2,1,0:T(8,128)} copy(f32[1,5,576,576]{3,2,1,0:T(8,128)} %bitcast.1) | data formatting | bytes 13271040

commit v3 on v2

--- a/solution.py
+++ b/solution.py
@@ -31,17 +31,19 @@
     strips = half + 2
     total = visits + groups * (half + 1) - half
     me = lax.axis_index('dp')
-    x, c = me // 2, me % 2
+    x, c = lax.div(me, 2), lax.rem(me, 2)
     partner = x * 2 + (1 - c)
 
+    upper_right = lax.rem(x + 1, chips) >= chips // 2
+
     def rightward(v):
-        return (v % 2 == 0) == ((x + 1) % chips >= chips // 2)
+        return (lax.rem(v, 2) == 0) == upper_right
 
     def dest(v):
         side = jnp.where(rightward(v), 1, chips - 1)
         off = jnp.where(v < 2, 2, jnp.where(v < far, side, 0))
-        core = select(v, (0, 1, 0, 0, 1, 1, 0, 1))
-        chip = (x + off) % chips
+        core = jnp.where(jnp.logical_or(jnp.logical_or(v == 1, v == 7), jnp.logical_or(v == 4, v == 5)), 1, 0)
+        chip = lax.rem(x + off, chips)
         return chip * 2 + core, core
 
     def slots_of(p):
@@ -49,15 +51,16 @@
 
     def via_plus(p, s):
         masks = select(p, (0b010100, 0b010101, 0b101010, 0b110110, 0b010110, 0b001011, 0b000100, 0b010100))
-        return masks // select(s, (1, 2, 4, 8, 16, 32)) % 2 == 1
+        return lax.rem(lax.div(masks, select(s, (1, 2, 4, 8, 16, 32))), 2) == 1
 
     def strip_at(v, i):
-        return jnp.where(v < far, jnp.where(i == slots_of(dest(v)[0]), 0, i + 1), i)
+        swapped = jnp.where(i < 2, 1 - i, i)
+        return jnp.where(v < 2, jnp.where(i == slots_of(dest(v)[0]), 0, i + 1), jnp.where(v < far, swapped, i))
 
     def following(v, s):
         nt = slots_of(dest(v)[0])
         paired = jnp.logical_and(v >= 2, v < far)
-        first = v % 2 == 0
+        first = lax.rem(v, 2) == 0
         mate = jnp.where(first, v + 1, v - 1)
         mate_s = jnp.where(first, s, s + 1)
         take_mate = jnp.logical_and(paired, mate_s <= slots_of(dest(mate)[0]))
@@ -90,7 +93,7 @@
     def start_lhs(v):
         p, _ = dest(v)
         pltpu.make_async_copy(
-            a_ref.at[pl.ds(pl.multiple_of(p * rows, 64), rows)], lhs.at[v % 2], lhs_sem.at[v % 2]
+            a_ref.at[pl.ds(pl.multiple_of(p * rows, 64), rows)], lhs.at[lax.rem(v, 2)], lhs_sem.at[lax.rem(v, 2)]
         ).start()
 
     def start_rhs(v, s, slot):
@@ -98,13 +101,13 @@
 
         @pl.when(s > 0)
         def _():
-            q = (p - (s - 1) + groups) % groups
+            q = lax.rem(p - (s - 1) + groups, groups)
             pltpu.make_async_copy(
                 a_ref.at[pl.ds(pl.multiple_of(q * rows, 64), MAIN)], rhs.at[slot], rhs_sem.at[slot]
             ).start()
 
         def piece(t, k):
-            q = (p - t + groups) % groups
+            q = lax.rem(p - t + groups, groups)
             pltpu.make_async_copy(
                 a_ref.at[pl.ds(pl.multiple_of(q * rows + MAIN, 64), rest)],
                 rhs.at[slot, pl.ds(k * rest, rest)],
@@ -124,7 +127,7 @@
     def signal_credit(kr, received):
         @pl.when(kr + DLAND < received)
         def _():
-            pl.semaphore_signal(credit.at[kr % DLAND], inc=1, device_id={'dp': partner}, device_id_type=pl.DeviceIdType.MESH)
+            pl.semaphore_signal(credit.at[lax.rem(kr, DLAND)], inc=1, device_id={'dp': partner}, device_id_type=pl.DeviceIdType.MESH)
 
     own = me
     received = total - (slots_of(own) + 1)
@@ -155,13 +158,13 @@
 
     def after(v, s, slot, kt, kr):
         p, core = dest(v)
-        k = kr % DLAND
+        k = lax.rem(kr, DLAND)
         mine = pl.ds(pl.multiple_of(c * hrows, 8), hrows)
         other = pl.ds(pl.multiple_of((1 - c) * hrows, 8), hrows)
         plus = via_plus(p, s)
         right = rightward(v)
         routed = on_route(v, p, s)
-        hop = jnp.where(plus, (x + chips - 1) % chips, (x + 1) % chips)
+        hop = lax.rem(x + jnp.where(plus, chips - 1, 1), chips)
         target = jnp.where(v < 2, hop * 2 + c, p)
         place = jnp.where(
             v < 2,
@@ -200,7 +203,7 @@
                     ).start()
 
                 if width == MAIN:
-                    ring = kt % RING
+                    ring = lax.rem(kt, RING)
 
                     @pl.when(kt >= RING)
                     def _():
@@ -234,10 +237,23 @@
                     def _():
                         pltpu.make_async_copy(fin, fin, fin_sem).wait()
 
-                    @pl.when(t <= p)
+                    @pl.when(t == 0)
+                    def _():
+                        def part(top, bottom, left, right):
+                            at = (slice(top, bottom), slice(left, right))
+                            return res[(slot, *at)] + dland[(k, *at)] + (rbuf[(0, *at)] + rbuf[(1, *at)])
+
+                        lower = part(256, rows, 0, 256)
+                        fin[0:256, 0:256] = part(0, 256, 0, 256)
+                        fin[256:rows, 0:256] = lower
+                        fin[0:256, 256:MAIN] = lower[0:256].T
+                        fin[256:rows, 256:MAIN] = part(256, rows, 256, MAIN)
+                        fin[:, pl.ds(MAIN, rest)] = remf[:, pl.ds(0, rest)]
+
+                    @pl.when(jnp.logical_and(t > 0, t <= p))
                     def _():
                         fin[:, cols] = whole()
-                        for i in range(half + 1):
+                        for i in range(1, half + 1):
                             @pl.when(t == i)
                             def _():
                                 fin[:, pl.ds(MAIN, rest)] = remf[:, pl.ds(i * rest, rest)]
@@ -245,7 +261,7 @@
                     @pl.when(t > p)
                     def _():
                         fin[pl.ds(0, MAIN), :] = whole().T
-                        for i in range(half + 1):
+                        for i in range(1, half + 1):
                             @pl.when(t == i)
                             def _():
                                 pair = remf[:, pl.ds(i // 2 * 128, 128)].T
@@ -287,7 +303,7 @@
         v, i, pv, pi, kt, ks, kr = carry
         p, core = dest(v)
         s, ps = strip_at(v, i), strip_at(pv, pi)
-        slot = g % 2
+        slot = lax.rem(g, 2)
         nv, ni = following(v, i)
 
         for width, cond in widths(p, s):
@@ -308,24 +324,37 @@
         def _():
             start_lhs(pv + 2)
 
+        held = lax.rem(v, 2)
+
         @pl.when(i == 0)
         def _():
-            pltpu.make_async_copy(lhs.at[v % 2], lhs.at[v % 2], lhs_sem.at[v % 2]).wait()
+            pltpu.make_async_copy(lhs.at[held], lhs.at[held], lhs_sem.at[held]).wait()
 
         @pl.when(g > 0)
         def _():
             before(pv, ps)
 
-        for width, cond in widths(p, s):
+        def product(width, top=0, left=0):
+            res[slot, top:rows, left:width] = lax.dot_general(
+                lhs[held, top:rows], rhs[slot, left:width], (((1,), (1,)), ((), ())), preferred_element_type=jnp.float32
+            )
+
+        @pl.when(s > 1)
+        def _():
+            product(MAIN)
+
+        @pl.when(s == 1)
+        def _():
+            product(256)
+            product(MAIN, 256, 256)
+
+        for width, cond in widths(p, s)[1:]:
             @pl.when(cond)
             def _():
-                res[slot, :, pl.ds(0, width)] = lax.dot_general(
-                    lhs[v % 2], rhs[slot, pl.ds(0, width)], (((1,), (1,)), ((), ())),
-                    preferred_element_type=jnp.float32,
-                )
+                product(width)
 
         gives = jnp.logical_or(v < far, core != c)
-        k = ks % DLAND
+        k = lax.rem(ks, DLAND)
 
         @pl.when(jnp.logical_and(gives, ks >= DLAND))
         def _():

time: 281 us -> 256 us (0.911)
  the two profiles are of different devices: /device:TPU:113 before, /device:TPU:117 now
where the time goes in v3:
time: 256 us
  Pallas kernels  249 us (97%)
  local copies, waits for them, and re-layouts  6.63 us (3%)
    pallas_call x1, Pallas kernels, local_gram(): pl.pallas_call(functools.partial(kernel, groups), out_shape=(jax.ShapeDty...  249 us
    unnamed x1, local copies, waits for them, and re-layouts  6.63 us

profile of v3, /device:TPU:117, one launch (start us, length us, event | category | flops | bytes accessed | tf_op | source)
XLA Modules:
  0.0 256.0 jit_solution(7679403806874924801)
XLA Ops:
  0.0 249.3 %gram_reduce.1 = (f32[5,576,576]{2,1,0:T(8,128)}, f32[48,288,512]{2,1,0:T(8,128)}) custom-call(bf16[4608,8192]{1,0:T(8,128)(2,1)} %a_ref.1), custom_call_target="tpu_custom_call" | custom-call | tf_op jit(solution)/shard_map/gram_reduce/pallas_call | solution.py:422
  249.3 6.6 %copy.3 = f32[1,5,576,576]{3,2,1,0:T(8,128)} copy(f32[1,5,576,576]{3,2,1,0:T(8,128)} %bitcast.1) | data formatting | bytes 13271040
